TPU v7x, 32 devices: a whole 2x2x4 slice. The times are simulated.
32 devices in a mesh: leaf: 8 (over z, y), rhs: 4 (over x, core).
Axes of the slice: x: 2, y: 2, z: 4, core: 2. Of those that a mesh axis runs over, the one named last changes fastest.
Arguments:
- right_sides: float32 [64, 8192], P('rhs', 'leaf'), may hold values from -8 to 8
- leaf_inverse: float32 [8192, 1024], P('leaf', 'rhs'), may hold values from -1 to 5, as said below
- bases: bfloat16 [3, 128, 8192], P(None, None, 'leaf'), may hold values from -1 to 1
- ordering: int32 [8, 1024], P('leaf'), may hold values from 0 to 1023, as said below
Outputs:
- solution: float32 [64, 8192], P('rhs', 'leaf')
Inputs may be any that keep to these rules, and one draw needn't show every extreme that they name: `leaf_inverse`: each leaf's block of 1024 rows is symmetric positive definite. `ordering`: each row is a permutation of 0 to 1023.
All inputs are finite; a program needn't handle non-finite values.
Results may differ from a plain program's by a relative error of at most 0.0003.
Values sent between devices are 32-bit elements; how exact they have to be, the bound alone decides.
A program may use at most 64 MiB of HBM per device.

v0:
```python
import functools

import jax
import jax.numpy as jnp
from jax import lax
from jax.experimental import pallas as pl
from jax.experimental.pallas import tpu as pltpu
from jax.sharding import PartitionSpec as P

F32 = jnp.float32
BF16 = jnp.bfloat16
NN = (((1,), (0,)), ((), ()))
NT = (((1,), (1,)), ((), ()))
STEP = 32
TILE = 8


def split(value, pieces):
    parts = []
    for _ in range(pieces):
        head = value.astype(BF16)
        parts.append(head)
        value = value - head.astype(F32)
    return parts


def dot(left, right, dims):
    return lax.dot_general(left, right, dims, preferred_element_type=F32)


def fine(left, right, dims):
    return lax.dot_general(
        left, right, dims, precision=lax.Precision.HIGHEST, preferred_element_type=F32
    )


def inverse(matrix):
    size = matrix.shape[0]
    lane = lax.broadcasted_iota(jnp.int32, (1, size), 1)
    row_of = lax.broadcasted_iota(jnp.int32, (TILE, 1), 0)

    def block(_, a):
        for k in range(0, STEP, 2):
            first, second = a[k : k + 1], a[k + 1 : k + 2]
            a00 = jnp.broadcast_to(a[k : k + 1, k : k + 1], (1, size))
            a01 = jnp.broadcast_to(a[k : k + 1, k + 1 : k + 2], (1, size))
            a10 = jnp.broadcast_to(a[k + 1 : k + 2, k : k + 1], (1, size))
            a11 = jnp.broadcast_to(a[k + 1 : k + 2, k + 1 : k + 2], (1, size))
            scale = 1.0 / (a00 * a11 - a01 * a10)
            at0, at1 = lane == k, lane == k + 1
            first = jnp.where(at0, 1.0, jnp.where(at1, 0.0, first))
            second = jnp.where(at0, 0.0, jnp.where(at1, 1.0, second))
            new0 = (a11 * first - a01 * second) * scale
            new1 = (a00 * second - a10 * first) * scale
            col0, col1 = a[:, k : k + 1], a[:, k + 1 : k + 2]
            kept = jnp.where(at0 | at1, 0.0, a)
            a = kept - col0 * new0 - col1 * new1
            base = k // TILE * TILE
            rows = a[base : base + TILE]
            rows = jnp.where(row_of == k - base, new0, rows)
            rows = jnp.where(row_of == k + 1 - base, new1, rows)
            before = [a[:base]] if base else []
            a = jnp.concatenate(before + [rows, a[base + TILE :]], 0)
        a = jnp.concatenate([a[STEP:], a[:STEP]], 0)
        return pltpu.roll(a, size - STEP, 1)

    return lax.fori_loop(0, size // STEP, block, matrix)


def plan(leaves, groups, levels, rank, rows):
    early = [("c0", rank)]
    late = []
    for j in range(levels):
        height = (levels - j) * rank
        if j == 1:
            early.append(("c1", rank))
        if j < 2:
            height -= rank
        if height:
            (late if j else early).append((f"m{j}", height))
    early.append(("t0", rows))
    if levels > 1:
        late.append(("t1", (levels - 1) * rows))
    return early, late


def other(index, bit):
    return index + bit - 2 * bit * ((index // bit) % 2)


def kernel(cfg, rs_ref, g_ref, b_ref, ord_ref, out_ref, *scratch):
    leaves, groups, levels, rank, own_rows, points, piece = cfg
    rows = groups * own_rows
    early, late = plan(leaves, groups, levels, rank, rows)
    early, late = [name for name, _ in early], [name for name, _ in late]
    names = early + late
    ref = dict(zip(scratch_names(cfg), scratch))
    leaf, position = lax.axis_index("leaf"), lax.axis_index("rhs")
    mesh_id = pl.DeviceIdType.MESH

    def at(leaf_index, rhs_index):
        return {"leaf": leaf_index, "rhs": rhs_index}

    rhs_peers = [lax.rem(position + k, groups) for k in range(1, groups)]
    mate = other(position, 1)
    half = lax.rem(position, 2)
    chips = [(leaf, lax.rem(position + k, groups)) for k in range(2, groups, 2)]
    chips += [(other(leaf, 1), lax.rem(position + k, groups)) for k in range(0, groups, 2)]
    greeted = [(leaf, p) for p in rhs_peers]
    greeted += chips[groups // 2 - 1 :]
    greeted += [(other(leaf, 1 << h), position) for h in range(1, levels)]

    barrier = pltpu.get_barrier_semaphore()
    for target in greeted:
        pl.semaphore_signal(barrier, inc=1, device_id=at(*target), device_id_type=mesh_id)

    def remote(src, dst, sems, slot, target):
        return pltpu.make_async_remote_copy(
            src_ref=src,
            dst_ref=dst,
            send_sem=ref[sems + "_s"].at[slot],
            recv_sem=ref[sems + "_r"].at[slot],
            device_id=at(*target),
            device_id_type=mesh_id,
        )

    g_parts = split(g_ref[...], 3)
    for k, part in enumerate(g_parts):
        ref[f"g{k}"][...] = part
    bases = b_ref[...].reshape(levels * rank, points)
    solved = dot(bases, g_parts[0], NN) + (dot(bases, g_parts[1], NN) + dot(bases, g_parts[2], NN))
    ref["y"][...] = solved
    own_cols = pl.ds(pl.multiple_of(position * piece, piece), piece)
    bases_own = b_ref[:, :, own_cols].reshape(levels * rank, piece)
    gram = sum(dot(part, bases_own, NT) for part in reversed(split(solved, 3)))
    for j in range(levels):
        column = gram[j * rank :, j * rank : (j + 1) * rank]
        if j < 2:
            ref[f"part_c{j}"][...] = column[:rank]
            column = column[rank:]
        if column.shape[0]:
            ref[f"part_m{j}"][...] = column

    pl.semaphore_wait(barrier, len(greeted))

    def halves(buffer, which):
        count = buffer.shape[0] // 2
        return buffer.at[pl.ds(pl.multiple_of(which * count, count), count)]

    def fold_start(name):
        slot = names.index(name)
        copy = remote(
            halves(ref["part_" + name], 1 - half), ref["fold_" + name], "fold", slot, (leaf, mate)
        )
        copy.start()
        return copy

    def spread_start(name, fold):
        fold.wait_recv()
        slot = names.index(name)
        ref["chip_" + name][...] = halves(ref["part_" + name], half)[...] + ref["fold_" + name][...]
        copies = []
        for k, target in enumerate(chips):
            copy = remote(
                ref["chip_" + name],
                ref["peer_" + name].at[k],
                "peer",
                slot * len(chips) + k,
                target,
            )
            copy.start()
            copies.append(copy)
        return copies

    def join_start(name, copies):
        for copy in copies:
            copy.wait_recv()
        total = ref["chip_" + name][...]
        for k in range(len(copies)):
            total = total + ref["peer_" + name][k]
        halves(ref["full_" + name], half)[...] = total
        slot = names.index(name)
        copy = remote(
            halves(ref["full_" + name], half),
            halves(ref["full_" + name], half),
            "join",
            slot,
            (leaf, mate),
        )
        copy.start()
        return copy

    grams = [name for name in names if not name.startswith("t")]
    folds = {name: fold_start(name) for name in grams}

    tile = rank
    order = ord_ref[...]

    def one_hot(i, carry):
        start = pl.multiple_of(i * tile, tile)
        index = lax.broadcasted_iota(jnp.int32, (tile, points), 0) + start
        ref["perm"][pl.ds(start, tile), :] = jnp.where(index == order, 1.0, 0.0).astype(BF16)
        return carry

    lax.fori_loop(0, points // tile, one_hot, 0)
    spreads = {"c0": spread_start("c0", folds["c0"])}
    moved = dot(jnp.concatenate(split(rs_ref[...], 3), 0), ref["perm"][...], NN)
    ref["tree"][...] = (moved[:own_rows] + moved[own_rows : 2 * own_rows]) + moved[2 * own_rows :]
    pieces = []
    for k, peer in enumerate(rhs_peers):
        copy = remote(
            ref["tree"].at[:, pl.ds(pl.multiple_of(peer * piece, piece), piece)],
            ref["cols"].at[position],
            "cols",
            k,
            (leaf, peer),
        )
        copy.start()
        pieces.append(copy)
    ref["cols"][position] = ref["tree"][:, own_cols]
    for name in early[1:]:
        if name in grams:
            spreads[name] = spread_start(name, folds[name])
    for copy in pieces:
        copy.wait_recv()
    term = fine(ref["cols"][...].reshape(rows, piece), ref["y"][...], NT)
    ref["part_t0"][...] = term[:, :rank]
    folds["t0"] = fold_start("t0")
    for j in range(1, levels):
        ref["part_t1"][(j - 1) * rows : j * rows] = term[:, j * rank : (j + 1) * rank]
    if levels > 1:
        folds["t1"] = fold_start("t1")
    spreads["t0"] = spread_start("t0", folds["t0"])
    for name in late:
        spreads[name] = spread_start(name, folds[name])
    sent = []
    for k, peer in enumerate(rhs_peers):
        copy = remote(ref["tree"], ref["rs"].at[position], "rs", k, (leaf, peer))
        copy.start()
        sent.append(copy)
    ref["rs"][position] = ref["tree"][...]

    def plain_term():
        for copy in sent:
            copy.wait_recv()
        gathered = ref["rs"][...].reshape(rows, points)
        stack = jnp.concatenate(split(gathered, 3), 0)
        by_0 = dot(stack, ref["g0"][...], NN)
        by_1 = dot(stack[: 2 * rows], ref["g1"][...], NN)
        by_2 = dot(stack[:rows], ref["g2"][...], NN)
        ref["x"][...] = by_0[:rows] + (
            (by_0[rows : 2 * rows] + by_1[:rows]) + (by_0[2 * rows :] + by_1[rows:] + by_2)
        )

    joins = {"c0": join_start("c0", spreads["c0"])}
    eye = (
        lax.broadcasted_iota(jnp.int32, (rank, rank), 0)
        == lax.broadcasted_iota(jnp.int32, (rank, rank), 1)
    ).astype(F32)
    joins["c0"].wait_recv()

    level_copies = {}
    weights = []
    slots = iter(range(levels * levels * 2))

    def level_start(h, j, which, start, value):
        span = pl.ds(start, value.shape[0])
        ref[f"send{h}_{j}"][span, :] = value
        copy = remote(
            ref[f"send{h}_{j}"].at[span],
            ref[f"get{h}_{j}"].at[span],
            "level",
            next(slots),
            (other(leaf, 1 << h), position),
        )
        copy.start()
        level_copies[h, j, which] = copy

    def level_value(h, j, start):
        return ref[f"send{h}_{j}"][start:] + ref[f"get{h}_{j}"][start:]

    for h in range(levels):
        if h == 0:
            capacity = ref["full_c0"][...]
        else:
            level_copies[h, h, 0].wait_recv()
            capacity = ref[f"send{h}_{h}"][:rank] + ref[f"get{h}_{h}"][:rank]
        inverted = inverse(capacity + eye)
        if h == 0:
            for name in early[1:]:
                joins[name] = join_start(name, spreads[name])
            for name in early[1:]:
                joins[name].wait_recv()
            rest = ref["full_t0"][...]
            if levels > 1:
                rest = jnp.concatenate([ref["full_m0"][...], rest], 0)
                head = ref["full_c1"][...]
        else:
            level_copies[h, h, 1].wait_recv()
            rest = level_value(h, h, rank)
            if h + 1 < levels:
                level_copies[h, h + 1, 1].wait_recv()
                following = level_value(h, h + 1, 0)
                head, tail = following[:rank], following[rank:]
        if h + 1 < levels:
            first = fine(rest[:rank], inverted, NN)
            level_start(h + 1, h + 1, 0, 0, head - fine(first, rest[:rank], NT))
            weight = jnp.concatenate([first, fine(rest[rank:], inverted, NN)], 0)
        else:
            weight = fine(rest, inverted, NN)
        weights.append(weight)
        if h == 0:
            for name in late:
                joins[name] = join_start(name, spreads[name])
            for name in late:
                joins[name].wait_recv()
        for j in range(h + 1, levels):
            offset = (j - h - 1) * rank
            start = rank if j == h + 1 else 0
            if h == 0:
                column = ref["full_t1"][(j - 1) * rows : j * rows]
                if f"m{j}" in names:
                    column = jnp.concatenate([ref[f"full_m{j}"][...], column], 0)
            elif j == h + 1:
                column = tail
            else:
                level_copies[h, j, 1].wait_recv()
                column = level_value(h, j, 0)
            update = fine(weight[offset + start :], rest[offset : offset + rank], NT)
            level_start(h + 1, j, 1, start, column - update)
        if h == max(levels - 2, 0):
            plain_term()

    coefficients = [None] * levels
    for h in reversed(range(levels)):
        value = weights[h][(levels - 1 - h) * rank :]
        for j in range(h + 1, levels):
            offset = (j - h - 1) * rank
            value = value - fine(coefficients[j], weights[h][offset : offset + rank], NN)
        coefficients[h] = value
    answer = ref["x"][...] - fine(jnp.concatenate(coefficients, 1), ref["y"][...], NN)
    ref["answer"][...] = answer.reshape(groups, own_rows, piece)
    last = []
    for k, peer in enumerate(rhs_peers):
        copy = remote(ref["answer"].at[peer], ref["final"].at[position], "last", k, (leaf, peer))
        copy.start()
        last.append(copy)
    ref["final"][position] = ref["answer"][position]
    for copy in last:
        copy.wait_recv()
    tree_rows = jnp.concatenate([ref["final"][k] for k in range(groups)], 1)
    moved = dot(jnp.concatenate(split(tree_rows, 3), 0), ref["perm"][...], NT)
    out_ref[...] = moved[:own_rows] + (moved[own_rows : 2 * own_rows] + moved[2 * own_rows :])

    for copy in pieces + sent + last + list(folds.values()) + list(joins.values()):
        copy.wait_send()
    for copies in spreads.values():
        for copy in copies:
            copy.wait_send()
    for copy in level_copies.values():
        copy.wait_send()


def scratch_list(cfg):
    leaves, groups, levels, rank, own_rows, points, piece = cfg
    rows = groups * own_rows
    early, late = plan(leaves, groups, levels, rank, rows)
    units = early + late
    chips = groups - 1
    items = [
        ("y", pltpu.VMEM((levels * rank, piece), F32)),
        ("x", pltpu.VMEM((rows, piece), F32)),
        ("rs", pltpu.VMEM((groups, own_rows, points), F32)),
        ("tree", pltpu.VMEM((own_rows, points), F32)),
        ("cols", pltpu.VMEM((groups, own_rows, piece), F32)),
        ("g0", pltpu.VMEM((points, piece), BF16)),
        ("g1", pltpu.VMEM((points, piece), BF16)),
        ("g2", pltpu.VMEM((points, piece), BF16)),
        ("perm", pltpu.VMEM((points, points), BF16)),
        ("answer", pltpu.VMEM((groups, own_rows, piece), F32)),
        ("final", pltpu.VMEM((groups, own_rows, piece), F32)),
    ]
    for name, height in units:
        items += [
            ("part_" + name, pltpu.VMEM((height, rank), F32)),
            ("fold_" + name, pltpu.VMEM((height // 2, rank), F32)),
            ("chip_" + name, pltpu.VMEM((height // 2, rank), F32)),
            ("peer_" + name, pltpu.VMEM((chips, height // 2, rank), F32)),
            ("full_" + name, pltpu.VMEM((height, rank), F32)),
        ]
    pairs = 0
    for h in range(1, levels):
        for j in range(h, levels):
            pairs += 1
            height = (levels - j) * rank + rows
            items.append((f"send{h}_{j}", pltpu.VMEM((height, rank), F32)))
            items.append((f"get{h}_{j}", pltpu.VMEM((height, rank), F32)))
    counts = {
        "rs": groups - 1,
        "cols": groups - 1,
        "last": groups - 1,
        "fold": len(units),
        "join": len(units),
        "peer": len(units) * chips,
        "level": max(1, 2 * pairs),
    }
    for name, count in counts.items():
        items.append((name + "_s", pltpu.SemaphoreType.DMA((count,))))
        items.append((name + "_r", pltpu.SemaphoreType.DMA((count,))))
    return items


def scratch_names(cfg):
    return [name for name, _ in scratch_list(cfg)]


def local(right_sides, leaf_inverse, bases, ordering):
    own_rows, points = right_sides.shape
    levels, rank = bases.shape[:2]
    cfg = (
        lax.axis_size("leaf"),
        lax.axis_size("rhs"),
        levels,
        rank,
        own_rows,
        points,
        leaf_inverse.shape[1],
    )
    return pl.pallas_call(
        functools.partial(kernel, cfg),
        out_shape=jax.ShapeDtypeStruct((own_rows, points), F32),
        in_specs=[pl.BlockSpec(memory_space=pltpu.VMEM)] * 4,
        out_specs=pl.BlockSpec(memory_space=pltpu.VMEM),
        scratch_shapes=[item for _, item in scratch_list(cfg)],
        compiler_params=pltpu.CompilerParams(collective_id=0, has_side_effects=True),
        name="tree_solve",
    )(right_sides, leaf_inverse, bases, ordering)


def solution(mesh):
    placed = (P("rhs", "leaf"), P("leaf", "rhs"), P(None, None, "leaf"), P("leaf", None))
    return jax.shard_map(
        local, mesh=mesh, in_specs=placed, out_specs=P("rhs", "leaf"), check_vma=False
    )
```

profile of v0, /device:TPU:0, one launch (start us, length us, event | category | flops | bytes accessed | tf_op | source)
XLA Modules:
  0.0 51.9 jit_solution(7214029706156762496)
XLA Ops:
  0.0 50.4 %tree_solve.1 = f32[16,1024]{1,0:T(8,128)} custom-call(f32[16,1024]{1,0:T(8,128)} %rs_ref.1, f32[1024,256]{1,0:T(8,128)} %g_ref.1, bf16[3,128,1024]{2,1,0:T(8,128)(2,1)} %b_ref.1, s32[1,1024]{1,0:T(1,128)} %ord_ref.1), custom_call_target="tpu_custom_call" | custom-call | tf_op jit(solution)/shard_map/tree_solve/pallas_call | solution.py:429
  50.4 1.5 %copy.6 = f32[16,1024]{1,0:T(8,128)} copy(f32[16,1024]{1,0:T(8,128)} %tree_solve.1) | data formatting | bytes 131072
where the time goes:
time: 52 us; the launch traced here: 51.9 us
  Pallas kernels  50.4 us (97%)
  local copies, waits for them, and re-layouts  1.47 us (3%)
    pallas_call x1, Pallas kernels, local(): pl.pallas_call(functools.partial(kernel, cfg), out_shape=jax.ShapeDtypeSt...  50.4 us
    unnamed x1, local copies, waits for them, and re-layouts  1.47 us

commit v1 on v0

--- a/solution.py
+++ b/solution.py
@@ -11,8 +11,7 @@
 BF16 = jnp.bfloat16
 NN = (((1,), (0,)), ((), ()))
 NT = (((1,), (1,)), ((), ()))
-STEP = 32
-TILE = 8
+PANEL = 16
 
 
 def split(value, pieces):
@@ -36,35 +35,46 @@
 
 def inverse(matrix):
     size = matrix.shape[0]
-    lane = lax.broadcasted_iota(jnp.int32, (1, size), 1)
-    row_of = lax.broadcasted_iota(jnp.int32, (TILE, 1), 0)
-
-    def block(_, a):
-        for k in range(0, STEP, 2):
-            first, second = a[k : k + 1], a[k + 1 : k + 2]
-            a00 = jnp.broadcast_to(a[k : k + 1, k : k + 1], (1, size))
-            a01 = jnp.broadcast_to(a[k : k + 1, k + 1 : k + 2], (1, size))
-            a10 = jnp.broadcast_to(a[k + 1 : k + 2, k : k + 1], (1, size))
-            a11 = jnp.broadcast_to(a[k + 1 : k + 2, k + 1 : k + 2], (1, size))
-            scale = 1.0 / (a00 * a11 - a01 * a10)
-            at0, at1 = lane == k, lane == k + 1
-            first = jnp.where(at0, 1.0, jnp.where(at1, 0.0, first))
-            second = jnp.where(at0, 0.0, jnp.where(at1, 1.0, second))
-            new0 = (a11 * first - a01 * second) * scale
-            new1 = (a00 * second - a10 * first) * scale
-            col0, col1 = a[:, k : k + 1], a[:, k + 1 : k + 2]
-            kept = jnp.where(at0 | at1, 0.0, a)
-            a = kept - col0 * new0 - col1 * new1
-            base = k // TILE * TILE
-            rows = a[base : base + TILE]
-            rows = jnp.where(row_of == k - base, new0, rows)
-            rows = jnp.where(row_of == k + 1 - base, new1, rows)
-            before = [a[:base]] if base else []
-            a = jnp.concatenate(before + [rows, a[base + TILE :]], 0)
-        a = jnp.concatenate([a[STEP:], a[:STEP]], 0)
-        return pltpu.roll(a, size - STEP, 1)
-
-    return lax.fori_loop(0, size // STEP, block, matrix)
+    count = size // PANEL
+    lane = lax.broadcasted_iota(jnp.int32, (PANEL, size), 1)
+    row = lax.broadcasted_iota(jnp.int32, (PANEL, size), 0)
+    zero = jnp.zeros((PANEL, size), F32)
+    panels = [matrix[i * PANEL : (i + 1) * PANEL] for i in range(count)]
+
+    def spread(panel, column):
+        return jnp.broadcast_to(panel[:, column : column + 1], (PANEL, size))
+
+    for i in range(count):
+        start = i * PANEL
+        inside = (lane >= start) & (lane < start + PANEL)
+        panel = panels[i]
+        columns = [spread(panel, start + k) for k in range(PANEL)]
+        ahead = i + 1 < count
+        if ahead:
+            next_columns = [spread(panels[i + 1], start + k) for k in range(PANEL)]
+        panel = jnp.where(inside, jnp.where(lane - start == row, 1.0, 0.0), panel)
+        for k in range(PANEL):
+            scale = 1.0 / columns[k][k : k + 1]
+            at = row == k
+            factor = jnp.where(at, -1.0, columns[k])
+            panel = jnp.where(at, 0.0, panel) - factor * (panel[k : k + 1] * scale)
+            for j in range(k + 1, PANEL):
+                pivot = columns[j][k : k + 1] * scale
+                columns[j] = jnp.where(at, 0.0, columns[j]) - factor * pivot
+        padded = jnp.concatenate([zero] * i + [panel] + [zero] * (count - 1 - i), 0)
+        update = fine(jnp.concatenate(panels, 0), padded, NN)
+        if ahead:
+            change = next_columns[0] * panel[0:1]
+            for k in range(1, PANEL):
+                change = change + next_columns[k] * panel[k : k + 1]
+        for j in range(count):
+            if j == i:
+                panels[j] = panel
+            else:
+                own = update[j * PANEL : (j + 1) * PANEL]
+                own = change if j == i + 1 else own
+                panels[j] = jnp.where(inside, 0.0, panels[j]) - own
+    return jnp.concatenate(panels, 0)
 
 
 def plan(leaves, groups, levels, rank, rows):

time: 52 us -> 46.6 us (0.90)
  Pallas kernels: 50.4 us -> 44.9 us
    pallas_call x1, Pallas kernels: 50.4 us -> 44.9 us  [local(): pl.pallas_call(functools.partial(kernel, cfg), out_shape=jax.ShapeDtypeSt...]
where the time goes in v1:
time: 46.6 us; the launch traced here: 46.4 us
  Pallas kernels  44.9 us (96%)
  local copies, waits for them, and re-layouts  1.47 us (3%)
    pallas_call x1, Pallas kernels, local(): pl.pallas_call(functools.partial(kernel, cfg), out_shape=jax.ShapeDtypeSt...  44.9 us
    unnamed x1, local copies, waits for them, and re-layouts  1.47 us

profile of v1, /device:TPU:0, one launch (start us, length us, event | category | flops | bytes accessed | tf_op | source)
XLA Modules:
  0.0 46.4 jit_solution(8763614762165250089)
XLA Ops:
  0.0 44.9 %tree_solve.1 = f32[16,1024]{1,0:T(8,128)} custom-call(f32[16,1024]{1,0:T(8,128)} %rs_ref.1, f32[1024,256]{1,0:T(8,128)} %g_ref.1, bf16[3,128,1024]{2,1,0:T(8,128)(2,1)} %b_ref.1, s32[1,1024]{1,0:T(1,128)} %ord_ref.1), custom_call_target="tpu_custom_call" | custom-call | tf_op jit(solution)/shard_map/tree_solve/pallas_call | solution.py:439
  44.9 1.5 %copy.6 = f32[16,1024]{1,0:T(8,128)} copy(f32[16,1024]{1,0:T(8,128)} %tree_solve.1) | data formatting | bytes 131072

commit v2 on v1

v2 whole, which is shorter than its diff:
```python
import functools

import jax
import jax.numpy as jnp
from jax import lax
from jax.experimental import pallas as pl
from jax.experimental.pallas import tpu as pltpu
from jax.sharding import PartitionSpec as P

F32 = jnp.float32
BF16 = jnp.bfloat16
NN = (((1,), (0,)), ((), ()))
NT = (((1,), (1,)), ((), ()))
PANEL = 16


def split(value, pieces):
    parts = []
    for _ in range(pieces):
        head = value.astype(BF16)
        parts.append(head)
        value = value - head.astype(F32)
    return parts


def dot(left, right, dims):
    return lax.dot_general(left, right, dims, preferred_element_type=F32)


def fine(left, right, dims):
    return lax.dot_general(
        left, right, dims, precision=lax.Precision.HIGHEST, preferred_element_type=F32
    )


def inverse(matrix, hooks):
    size = matrix.shape[0]
    count = size // PANEL
    lane = lax.broadcasted_iota(jnp.int32, (PANEL, size), 1)
    row = lax.broadcasted_iota(jnp.int32, (PANEL, size), 0)
    zero = jnp.zeros((PANEL, size), F32)
    panels = [matrix[i * PANEL : (i + 1) * PANEL] for i in range(count)]

    def spread(panel, column):
        return jnp.broadcast_to(panel[:, column : column + 1], (PANEL, size))

    for i in range(count):
        for hook in hooks.get(i, ()):
            hook()
        start = i * PANEL
        inside = (lane >= start) & (lane < start + PANEL)
        panel = panels[i]
        columns = [spread(panel, start + k) for k in range(PANEL)]
        ahead = i + 1 < count
        if ahead:
            next_columns = [spread(panels[i + 1], start + k) for k in range(PANEL)]
        panel = jnp.where(inside, jnp.where(lane - start == row, 1.0, 0.0), panel)
        for k in range(PANEL):
            scale = 1.0 / columns[k][k : k + 1]
            at = row == k
            factor = jnp.where(at, -1.0, columns[k])
            panel = jnp.where(at, 0.0, panel) - factor * (panel[k : k + 1] * scale)
            for j in range(k + 1, PANEL):
                pivot = columns[j][k : k + 1] * scale
                columns[j] = jnp.where(at, 0.0, columns[j]) - factor * pivot
        padded = jnp.concatenate([zero] * i + [panel] + [zero] * (count - 1 - i), 0)
        update = fine(jnp.concatenate(panels, 0), padded, NN)
        if ahead:
            change = next_columns[0] * panel[0:1]
            for k in range(1, PANEL):
                change = change + next_columns[k] * panel[k : k + 1]
        for j in range(count):
            if j == i:
                panels[j] = panel
            else:
                own = update[j * PANEL : (j + 1) * PANEL]
                own = change if j == i + 1 else own
                panels[j] = jnp.where(inside, 0.0, panels[j]) - own
    return jnp.concatenate(panels, 0)


def blocks_of(levels, first):
    later = [(i, first) for i in range(first + 1, levels)]
    for j in range(first + 1, levels):
        later += [(i, j) for i in range(j, levels)]
    return [(first, first)] + later


def direct_units(levels):
    units = {"c": [(0, 0)]}
    if levels > 1:
        units["a"] = [(1, 0), (1, 1)]
    if levels > 2:
        units["d"] = [(i, 0) for i in range(2, levels)]
    return units


def slow_units(levels):
    units = {}
    if levels > 2:
        units["e1"] = [(i, 1) for i in range(2, levels)]
    for j in range(2, levels):
        units[f"e{j}"] = [(i, j) for i in range(j, levels)]
    return units


def bits(count):
    return [1 << k for k in range(count.bit_length() - 1)]


def stages_of(name, groups):
    column = int(name[1:])
    stages = [(2, 0)] + [(0, bit) for bit in bits(groups)[1:]] + [(1, 0)]
    return stages + [(1 << h, 0) for h in range(2, column + 1)]


def other(index, bit):
    return index + bit - 2 * bit * ((index // max(bit, 1)) % 2)


def kernel(cfg, rs_ref, g_ref, b_ref, ord_ref, out_ref, *scratch):
    leaves, groups, levels, rank, own_rows, points, piece = cfg
    rows = groups * own_rows
    ref = dict(zip(scratch_names(cfg), scratch))
    leaf, position = lax.axis_index("leaf"), lax.axis_index("rhs")
    mesh_id = pl.DeviceIdType.MESH
    direct, slow = direct_units(levels), slow_units(levels)

    def at(leaf_index, rhs_index):
        return {"leaf": leaf_index, "rhs": rhs_index}

    rhs_peers = [lax.rem(position + k, groups) for k in range(1, groups)]
    mate = other(position, 1)
    half = lax.rem(position, 2)
    chips = [(leaf, lax.rem(position + k, groups)) for k in range(2, groups, 2)]
    across = [peer for _, peer in chips]
    chips += [(other(leaf, 1), lax.rem(position + k, groups)) for k in range(0, groups, 2)]
    greeted = [(leaf, p) for p in rhs_peers]
    greeted += chips[groups // 2 - 1 :]
    greeted += [(other(leaf, 1 << h), position) for h in range(1, levels)]

    barrier = pltpu.get_barrier_semaphore()
    for target in greeted:
        pl.semaphore_signal(barrier, inc=1, device_id=at(*target), device_id_type=mesh_id)

    started = []

    def send(src, dst, target):
        slot = len(started)
        copy = pltpu.make_async_remote_copy(
            src_ref=src,
            dst_ref=dst,
            send_sem=ref["sent"].at[slot],
            recv_sem=ref["received"].at[slot],
            device_id=at(*target),
            device_id_type=mesh_id,
        )
        copy.start()
        started.append(copy)
        return copy

    def halves(buffer, which):
        count = buffer.shape[0] // 2
        return buffer.at[pl.ds(pl.multiple_of(which * count, count), count)]

    flying = {}

    def fold(name):
        part = halves(ref["part_" + name], 1 - half)
        flying[name] = send(part, ref["fold_" + name], (leaf, mate))

    def folded(name):
        flying[name].wait_recv()
        return halves(ref["part_" + name], half)[...] + ref["fold_" + name][...]

    def join(name, total):
        own = halves(ref["full_" + name], half)
        own[...] = total
        flying[name] = send(own, own, (leaf, mate))

    def scatter(name):
        ref["chip_" + name][...] = folded(name)
        flying[name] = [
            send(ref["chip_" + name], ref["peer_" + name].at[k], target)
            for k, target in enumerate(chips)
        ]

    def gather(name):
        total = ref["chip_" + name][...]
        for k, copy in enumerate(flying[name]):
            copy.wait_recv()
            total = total + ref["peer_" + name][k]
        join(name, total)

    def joined(name):
        flying[name].wait_recv()

    def slow_step(name, stage):
        stages = stages_of(name, groups)
        if stage == 0:
            total = folded(name)
        else:
            flying[name].wait_recv()
            total = ref["pass_" + name][stage - 1] + ref["come_" + name][stage - 1]
        if stage == len(stages):
            join(name, total)
            return
        ref["pass_" + name][stage] = total
        leaf_bit, rhs_bit = stages[stage]
        target = (other(leaf, leaf_bit), other(position, rhs_bit))
        flying[name] = send(ref["pass_" + name].at[stage], ref["come_" + name].at[stage], target)

    todo = {}
    for name in slow:
        count = len(stages_of(name, groups))
        todo[name] = [functools.partial(slow_step, name, k) for k in range(count + 1)]
        todo[name].append(functools.partial(joined, name))

    def step(name, count=1):
        for _ in range(count):
            if todo.get(name):
                todo[name].pop(0)()

    def finish(name):
        while todo.get(name):
            step(name)

    g_parts = split(g_ref[...], 3)
    for k, part in enumerate(g_parts):
        ref[f"g{k}"][...] = part
    own_cols = pl.ds(pl.multiple_of(position * piece, piece), piece)
    bases_own = b_ref[:, :, own_cols].reshape(levels * rank, piece)
    own_y = ref["y"].at[position]

    def gram_of(first, last, width):
        left = b_ref[first:last].reshape((last - first) * rank, points)
        solved = dot(left, g_parts[0], NN) + (
            dot(left, g_parts[1], NN) + dot(left, g_parts[2], NN)
        )
        own_y[first * rank : last * rank] = solved
        right = bases_own[: width * rank]
        return sum(dot(part, right, NT) for part in reversed(split(solved, 3)))

    ref["part_c"][...] = gram_of(0, 1, 1)
    pl.semaphore_wait(barrier, len(greeted))
    fold("c")
    order = ord_ref[...]

    def one_hot(i, carry):
        start = pl.multiple_of(i * rank, rank)
        index = lax.broadcasted_iota(jnp.int32, (rank, points), 0) + start
        ref["perm"][pl.ds(start, rank), :] = jnp.where(index == order, 1.0, 0.0).astype(BF16)
        return carry

    lax.fori_loop(0, points // rank, one_hot, 0)
    moved = dot(jnp.concatenate(split(rs_ref[...], 3), 0), ref["perm"][...], NN)
    tree = (moved[:own_rows] + moved[own_rows : 2 * own_rows]) + moved[2 * own_rows :]
    for k in range(groups):
        ref["tree"][k] = tree[:, k * piece : (k + 1) * piece]
    scatter("c")
    pieces = []
    for peer in rhs_peers:
        pieces.append(send(ref["tree"].at[peer], ref["cols"].at[position], (leaf, peer)))
    ref["cols"][position] = ref["tree"][position]

    def part_store(gram, start, name, blocks):
        for k, (i, j) in enumerate(blocks):
            ref["part_" + name][k * rank : (k + 1) * rank] = gram[
                (i - start) * rank : (i - start + 1) * rank, j * rank : (j + 1) * rank
            ]

    if levels > 1:
        part_store(gram_of(1, 2, 2), 1, "a", direct["a"])
        fold("a")
    if levels > 2:
        gram = gram_of(2, levels, levels)
        later = {name: blocks for name, blocks in direct.items() if name not in "ca"}
        later |= slow
        for name, blocks in later.items():
            part_store(gram, 2, name, blocks)
        scatter("a")
        for name in later:
            fold(name)
    elif levels > 1:
        scatter("a")

    terms = []

    def term_part():
        for copy in pieces:
            copy.wait_recv()
        columns = ref["cols"][...].reshape(rows, piece)
        term = fine(columns, own_y[...], NT)
        for k in range(groups):
            ref["term"][k % 2, k // 2] = term[k * own_rows : (k + 1) * own_rows]
        terms.append(send(ref["term"].at[1 - half], ref["term_fold"], (leaf, mate)))

    def term_cross():
        terms[0].wait_recv()
        ref["term_chip"][...] = ref["term"][half] + ref["term_fold"][...]
        for k, peer in enumerate(across):
            source = ref["term_chip"].at[lax.div(peer, 2)]
            terms.append(send(source, ref["term_get"].at[k], (leaf, peer)))

    def term_sum():
        total = ref["term_chip"][lax.div(position, 2)]
        for k, copy in enumerate(terms[1:]):
            copy.wait_recv()
            total = total + ref["term_get"][k]
        ref["term_pass"][...] = total
        terms.append(send(ref["term_pass"], ref["term_come"], (other(leaf, 1), position)))

    def term_joined():
        terms[-1].wait_recv()

    plain = []

    def plain_part():
        stack = jnp.concatenate(split(ref["cols"][...].reshape(rows, piece), 3), 0)
        by_0 = dot(stack, ref["g0"][...], NT)
        by_1 = dot(stack[: 2 * rows], ref["g1"][...], NT)
        by_2 = dot(stack[:rows], ref["g2"][...], NT)
        value = by_0[:rows] + (
            (by_0[rows : 2 * rows] + by_1[:rows]) + (by_0[2 * rows :] + by_1[rows:] + by_2)
        )
        for k in range(groups):
            ref["plain"][k % 2, k // 2] = value[k * own_rows : (k + 1) * own_rows]
        plain.append(send(ref["plain"].at[1 - half], ref["plain_fold"], (leaf, mate)))

    def plain_cross():
        plain[0].wait_recv()
        ref["plain_chip"][...] = ref["plain"][half] + ref["plain_fold"][...]
        for k, peer in enumerate(across):
            source = ref["plain_chip"].at[lax.div(peer, 2)]
            plain.append(send(source, ref["plain_get"].at[k], (leaf, peer)))

    def plain_sum():
        total = ref["plain_chip"][lax.div(position, 2)]
        for k, copy in enumerate(plain[1:]):
            copy.wait_recv()
            total = total + ref["plain_get"][k]
        ref["x"][...] = total

    solved_copies, relays = [], []

    def solved_send():
        for peer in across:
            solved_copies.append(send(own_y, own_y, (leaf, peer)))
        relays.append(send(own_y, own_y, (leaf, mate)))

    def solved_relay():
        for k, copy in enumerate(solved_copies):
            copy.wait_recv()
            source = lax.rem(position + groups - 2 * (k + 1), groups)
            slot = ref["y"].at[source]
            relays.append(send(slot, slot, (leaf, mate)))

    def solved_done():
        for copy in relays:
            copy.wait_recv()
        for k in range(groups):
            for p, part in enumerate(split(ref["y"][k], 2)):
                ref[f"y{p}"][:, k * piece : (k + 1) * piece] = part

    eye = (
        lax.broadcasted_iota(jnp.int32, (rank, rank), 0)
        == lax.broadcasted_iota(jnp.int32, (rank, rank), 1)
    ).astype(F32)
    linear = {}
    for name, blocks in [*direct.items(), *slow.items()]:
        for k, block in enumerate(blocks):
            linear[block] = (name, k * rank)
    place = {}
    for h in range(1, levels):
        for k, block in enumerate(blocks_of(levels, h)):
            place[h, block] = k * rank

    def linear_value(block):
        name, start = linear[block]
        return ref["full_" + name][start : start + rank]

    def carried(h, block):
        start = place[h, block]
        span = slice(start, start + rank)
        return ref[f"send{h}"][span] + ref[f"get{h}"][span]

    def block_value(h, block):
        if h == 0:
            return linear_value(block)
        value = carried(h, block)
        return value if block == (1, 1) else value + linear_value(block)

    def term_value(h, j):
        if h == 0:
            span = slice(j * rank, (j + 1) * rank)
            return ref["term_pass"][:, span] + ref["term_come"][:, span]
        start = (j - h) * own_rows
        span = slice(start, start + own_rows)
        return ref[f"tsend{h}"][span] + ref[f"tget{h}"][span]

    level_copies = {}

    def level_send(h, part, start, stop):
        span = pl.ds(start, stop - start)
        level_copies[h, part] = send(
            ref[f"send{h}"].at[span], ref[f"get{h}"].at[span], (other(leaf, 1 << h), position)
        )

    def level_wait(h, part):
        copy = level_copies.pop((h, part), None)
        if copy is not None:
            copy.wait_recv()

    inverses = [None] * levels
    below = [None] * levels
    weights = {}
    term_weights = {}

    def level_terms(h):
        if h:
            level_wait(h, "terms")
        term_weights[h] = fine(term_value(h, h), inverses[h], NN)
        if h + 1 < levels:
            for k, j in enumerate(range(h + 1, levels)):
                change = fine(term_weights[h], below[h][j], NT)
                span = slice(k * own_rows, (k + 1) * own_rows)
                ref[f"tsend{h + 1}"][span] = term_value(h, j) - change
            level_copies[h + 1, "terms"] = send(
                ref[f"tsend{h + 1}"], ref[f"tget{h + 1}"], (other(leaf, 2 << h), position)
            )

    def level_change(h, block):
        i, j = block
        change = fine(weights[i, h], below[h][j], NT)
        if block == (1, 1):
            return linear_value(block) - change
        return carried(h, block) - change if h else -change

    def level_body(h):
        level_wait(h, "rest")
        target = ref[f"send{h + 1}"]
        blocks = blocks_of(levels, h + 1)
        split_at = levels - h - 1
        for part, first, last in (("column", 1, split_at), ("rest", split_at, len(blocks))):
            for k in range(first, last):
                target[k * rank : (k + 1) * rank] = level_change(h, blocks[k])
            if last > first:
                level_send(h + 1, part, first * rank, last * rank)

    for name in slow:
        step(name)
    gather("c")
    term_part()
    joined("c")
    hooks = {h: {} for h in range(levels)}
    hooks[0] = {
        1: [lambda: scatter("d")] if "d" in direct else [],
        2: [term_cross],
        4: [lambda: step("e1"), lambda: step("e2")],
        6: [lambda: gather("a")] if "a" in direct else [],
    }
    if levels > 2:
        hooks[1] = {
            3: [lambda: step("e1"), lambda: step("e2")],
            5: [term_joined, lambda: level_terms(0)],
            7: [lambda: finish("e1")],
        }
    for h in range(2, levels):
        hooks[h] = {}
    for h in range(levels):
        if h:
            level_wait(h, "head")
            if h > 1:
                finish(f"e{h}")
        inverses[h] = inverse(block_value(h, (h, h)) + eye, hooks[h])
        if h + 1 == levels:
            break
        if h == 0:
            joined("a")
        else:
            level_wait(h, "column")
            finish(f"e{h}")
        first = block_value(h, (h + 1, h))
        below[h] = {h + 1: first}
        weights[h + 1, h] = fine(first, inverses[h], NN)
        if h:
            level_wait(h, "rest")
        ref[f"send{h + 1}"][:rank] = level_change(h, (h + 1, h + 1))
        level_send(h + 1, "head", 0, rank)
        if h + 2 < levels:
            if h == 0:
                gather("d")
                step("e1")
                step("e2")
                joined("d")
            for i in range(h + 2, levels):
                below[h][i] = block_value(h, (i, h))
                weights[i, h] = fine(below[h][i], inverses[h], NN)
            level_body(h)
        if h == 0:
            term_sum()
            solved_send()
            plain_part()
        if h == levels - 2:
            if h == 0:
                term_joined()
                level_terms(0)
            step("e2")
        if h:
            level_terms(h)
        if h == levels - 2:
            hooks[h + 1] |= {0: [plain_cross], 1: [solved_relay], 6: [solved_done], 7: [plain_sum]}
    if levels == 1:
        term_sum()
        solved_send()
        plain_part()
        term_joined()
        plain_cross()
        solved_relay()
        plain_sum()
        solved_done()
    level_terms(levels - 1)

    coefficients = [None] * levels
    for h in reversed(range(levels)):
        value = term_weights[h]
        for j in range(h + 1, levels):
            value = value - fine(coefficients[j], weights[j, h], NN)
        coefficients[h] = value
    stack = jnp.concatenate(split(jnp.concatenate(coefficients, 1), 2), 0)
    by_0 = dot(stack, ref["y0"][...], NN)
    by_1 = dot(stack[:own_rows], ref["y1"][...], NN)
    tree_rows = ref["x"][...] - (by_0[:own_rows] + (by_0[own_rows:] + by_1))
    moved = dot(jnp.concatenate(split(tree_rows, 3), 0), ref["perm"][...], NT)
    out_ref[...] = moved[:own_rows] + (moved[own_rows : 2 * own_rows] + moved[2 * own_rows :])

    for copy in started:
        copy.wait_send()


def scratch_list(cfg):
    leaves, groups, levels, rank, own_rows, points, piece = cfg
    chips = groups - 1
    width = levels * rank
    direct, slow = direct_units(levels), slow_units(levels)
    items = [
        ("y", pltpu.VMEM((groups, width, piece), F32)),
        ("y0", pltpu.VMEM((width, points), BF16)),
        ("y1", pltpu.VMEM((width, points), BF16)),
        ("x", pltpu.VMEM((own_rows, points), F32)),
        ("tree", pltpu.VMEM((groups, own_rows, piece), F32)),
        ("cols", pltpu.VMEM((groups, own_rows, piece), F32)),
        ("plain", pltpu.VMEM((2, groups // 2, own_rows, points), F32)),
        ("plain_fold", pltpu.VMEM((groups // 2, own_rows, points), F32)),
        ("plain_chip", pltpu.VMEM((groups // 2, own_rows, points), F32)),
        ("plain_get", pltpu.VMEM((max(1, groups // 2 - 1), own_rows, points), F32)),
        ("term", pltpu.VMEM((2, groups // 2, own_rows, width), F32)),
        ("term_fold", pltpu.VMEM((groups // 2, own_rows, width), F32)),
        ("term_chip", pltpu.VMEM((groups // 2, own_rows, width), F32)),
        ("term_get", pltpu.VMEM((max(1, groups // 2 - 1), own_rows, width), F32)),
        ("term_pass", pltpu.VMEM((own_rows, width), F32)),
        ("term_come", pltpu.VMEM((own_rows, width), F32)),
        ("g0", pltpu.VMEM((points, piece), BF16)),
        ("g1", pltpu.VMEM((points, piece), BF16)),
        ("g2", pltpu.VMEM((points, piece), BF16)),
        ("perm", pltpu.VMEM((points, points), BF16)),
    ]
    count = 3 * groups + 4 * (levels - 1)
    for name, blocks in [*direct.items(), *slow.items()]:
        height = len(blocks) * rank
        items += [
            ("part_" + name, pltpu.VMEM((height, rank), F32)),
            ("fold_" + name, pltpu.VMEM((height // 2, rank), F32)),
            ("full_" + name, pltpu.VMEM((height, rank), F32)),
        ]
        if name in direct:
            count += 2 + chips
            items += [
                ("chip_" + name, pltpu.VMEM((height // 2, rank), F32)),
                ("peer_" + name, pltpu.VMEM((chips, height // 2, rank), F32)),
            ]
        else:
            stages = len(stages_of(name, groups))
            count += 2 + stages
            items += [
                ("pass_" + name, pltpu.VMEM((stages, height // 2, rank), F32)),
                ("come_" + name, pltpu.VMEM((stages, height // 2, rank), F32)),
            ]
    for h in range(1, levels):
        height = len(blocks_of(levels, h)) * rank
        items.append((f"send{h}", pltpu.VMEM((height, rank), F32)))
        items.append((f"get{h}", pltpu.VMEM((height, rank), F32)))
        height = (levels - h) * own_rows
        items.append((f"tsend{h}", pltpu.VMEM((height, rank), F32)))
        items.append((f"tget{h}", pltpu.VMEM((height, rank), F32)))
    items.append(("sent", pltpu.SemaphoreType.DMA((count,))))
    items.append(("received", pltpu.SemaphoreType.DMA((count,))))
    return items


def scratch_names(cfg):
    return [name for name, _ in scratch_list(cfg)]


def local(right_sides, leaf_inverse, bases, ordering):
    own_rows, points = right_sides.shape
    levels, rank = bases.shape[:2]
    cfg = (
        lax.axis_size("leaf"),
        lax.axis_size("rhs"),
        levels,
        rank,
        own_rows,
        points,
        leaf_inverse.shape[1],
    )
    return pl.pallas_call(
        functools.partial(kernel, cfg),
        out_shape=jax.ShapeDtypeStruct((own_rows, points), F32),
        in_specs=[pl.BlockSpec(memory_space=pltpu.VMEM)] * 4,
        out_specs=pl.BlockSpec(memory_space=pltpu.VMEM),
        scratch_shapes=[item for _, item in scratch_list(cfg)],
        compiler_params=pltpu.CompilerParams(collective_id=0, has_side_effects=True),
        name="tree_solve",
    )(right_sides, leaf_inverse, bases, ordering)


def solution(mesh):
    placed = (P("rhs", "leaf"), P("leaf", "rhs"), P(None, None, "leaf"), P("leaf", None))
    return jax.shard_map(
        local, mesh=mesh, in_specs=placed, out_specs=P("rhs", "leaf"), check_vma=False
    )
```

time: 46.6 us -> 39.4 us (0.85)
  Pallas kernels: 44.9 us -> 37.4 us
    pallas_call x1, Pallas kernels: 44.9 us -> 37.4 us  [local(): pl.pallas_call(functools.partial(kernel, cfg), out_shape=jax.ShapeDtypeSt...]
where the time goes in v2:
time: 39.4 us; the launch traced here: 38.8 us
  Pallas kernels  37.4 us (95%)
  local copies, waits for them, and re-layouts  1.47 us (4%)
    pallas_call x1, Pallas kernels, local(): pl.pallas_call(functools.partial(kernel, cfg), out_shape=jax.ShapeDtypeSt...  37.4 us
    unnamed x1, local copies, waits for them, and re-layouts  1.47 us

profile of v2, /device:TPU:0, one launch (start us, length us, event | category | flops | bytes accessed | tf_op | source)
XLA Modules:
  0.0 38.8 jit_solution(12603196630196698656)
XLA Ops:
  0.0 37.4 %tree_solve.1 = f32[16,1024]{1,0:T(8,128)} custom-call(f32[16,1024]{1,0:T(8,128)} %rs_ref.1, f32[1024,256]{1,0:T(8,128)} %g_ref.1, bf16[3,128,1024]{2,1,0:T(8,128)(2,1)} %b_ref.1, s32[1,1024]{1,0:T(1,128)} %ord_ref.1), custom_call_target="tpu_custom_call" | custom-call | tf_op jit(solution)/shard_map/tree_solve/pallas_call | solution.py:617
  37.4 1.5 %copy.6 = f32[16,1024]{1,0:T(8,128)} copy(f32[16,1024]{1,0:T(8,128)} %tree_solve.1) | data formatting | bytes 131072

commit v3 on v2

--- a/solution.py
+++ b/solution.py
@@ -1,4 +1,5 @@
 import functools
+import itertools
 
 import jax
 import jax.numpy as jnp
@@ -12,6 +13,8 @@
 NN = (((1,), (0,)), ((), ()))
 NT = (((1,), (1,)), ((), ()))
 PANEL = 16
+CHUNKS = 4
+POOL = 12
 
 
 def split(value, pieces):
@@ -104,21 +107,16 @@
     return units
 
 
-def bits(count):
-    return [1 << k for k in range(count.bit_length() - 1)]
-
-
-def stages_of(name, groups):
+def stages_of(name):
     column = int(name[1:])
-    stages = [(2, 0)] + [(0, bit) for bit in bits(groups)[1:]] + [(1, 0)]
-    return stages + [(1 << h, 0) for h in range(2, column + 1)]
+    return [1 << h for h in range(1, column + 1)] + [None]
 
 
 def other(index, bit):
     return index + bit - 2 * bit * ((index // max(bit, 1)) % 2)
 
 
-def kernel(cfg, rs_ref, g_ref, b_ref, ord_ref, out_ref, *scratch):
+def kernel(cfg, rs_hbm, g_hbm, b_hbm, ord_hbm, out_ref, *scratch):
     leaves, groups, levels, rank, own_rows, points, piece = cfg
     rows = groups * own_rows
     ref = dict(zip(scratch_names(cfg), scratch))
@@ -139,25 +137,57 @@
     greeted += chips[groups // 2 - 1 :]
     greeted += [(other(leaf, 1 << h), position) for h in range(1, levels)]
 
+    rs_ref, g_ref, b_ref, ord_ref = (ref[name] for name in ("rs", "g", "b", "ord"))
+    chunk = points // CHUNKS
+    moves = [(b_hbm.at[0], b_ref.at[0])]
+    for k in range(CHUNKS):
+        span = pl.ds(k * chunk, chunk)
+        moves.append((g_hbm.at[span], g_ref.at[span]))
+    moves += [(ord_hbm, ord_ref), (rs_hbm, rs_ref)]
+    if levels > 1:
+        later = pl.ds(1, levels - 1)
+        moves.append((b_hbm.at[later], b_ref.at[later]))
+    loads = [
+        pltpu.make_async_copy(src, dst, ref["sent"].at[POOL - 1 - k]) for k, (src, dst) in enumerate(moves)
+    ]
+    urgent = CHUNKS + 1
+    for load in loads[:urgent]:
+        load.start()
     barrier = pltpu.get_barrier_semaphore()
     for target in greeted:
         pl.semaphore_signal(barrier, inc=1, device_id=at(*target), device_id_type=mesh_id)
 
-    started = []
-
-    def send(src, dst, target):
-        slot = len(started)
+    pool = {}
+    turn = itertools.count()
+    slots = itertools.count()
+
+    def start(src, dst, target, receive, place):
+        if place in pool:
+            pool[place].wait_send()
         copy = pltpu.make_async_remote_copy(
             src_ref=src,
             dst_ref=dst,
-            send_sem=ref["sent"].at[slot],
-            recv_sem=ref["received"].at[slot],
+            send_sem=ref["sent"].at[place],
+            recv_sem=ref["received"].at[receive],
             device_id=at(*target),
             device_id_type=mesh_id,
         )
         copy.start()
-        started.append(copy)
+        pool[place] = copy
         return copy
+
+    def send(src, dst, target):
+        return start(src, dst, target, next(slots), next(turn) % POOL)
+
+    class Group:
+        def __init__(self, copies, landed):
+            receive = next(slots)
+            for src, dst, target in copies:
+                start(src, dst, target, receive, next(turn) % POOL)
+            self.wait = pltpu.make_async_copy(landed, landed, ref["received"].at[receive])
+
+        def wait_recv(self):
+            self.wait.wait()
 
     def halves(buffer, which):
         count = buffer.shape[0] // 2
@@ -180,15 +210,14 @@
 
     def scatter(name):
         ref["chip_" + name][...] = folded(name)
-        flying[name] = [
-            send(ref["chip_" + name], ref["peer_" + name].at[k], target)
-            for k, target in enumerate(chips)
-        ]
+        peers = ref["peer_" + name]
+        copies = [(ref["chip_" + name], peers.at[k], target) for k, target in enumerate(chips)]
+        flying[name] = Group(copies, peers)
 
     def gather(name):
         total = ref["chip_" + name][...]
-        for k, copy in enumerate(flying[name]):
-            copy.wait_recv()
+        flying[name].wait_recv()
+        for k in range(len(chips)):
             total = total + ref["peer_" + name][k]
         join(name, total)
 
@@ -196,23 +225,29 @@
         flying[name].wait_recv()
 
     def slow_step(name, stage):
-        stages = stages_of(name, groups)
+        stages = stages_of(name)
         if stage == 0:
             total = folded(name)
         else:
+            total = ref["pass_" + name][stage - 1]
             flying[name].wait_recv()
-            total = ref["pass_" + name][stage - 1] + ref["come_" + name][stage - 1]
+            for k in range(1 if stages[stage - 1] else len(chips)):
+                total = total + ref["come_" + name][stage - 1 + k]
         if stage == len(stages):
             join(name, total)
             return
         ref["pass_" + name][stage] = total
-        leaf_bit, rhs_bit = stages[stage]
-        target = (other(leaf, leaf_bit), other(position, rhs_bit))
-        flying[name] = send(ref["pass_" + name].at[stage], ref["come_" + name].at[stage], target)
+        if stages[stage] is None:
+            targets = chips
+        else:
+            targets = [(other(leaf, stages[stage]), position)]
+        own, landed = ref["pass_" + name].at[stage], ref["come_" + name]
+        copies = [(own, landed.at[stage + k], target) for k, target in enumerate(targets)]
+        flying[name] = Group(copies, landed.at[pl.ds(stage, len(targets))])
 
     todo = {}
     for name in slow:
-        count = len(stages_of(name, groups))
+        count = len(stages_of(name))
         todo[name] = [functools.partial(slow_step, name, k) for k in range(count + 1)]
         todo[name].append(functools.partial(joined, name))
 
@@ -225,25 +260,39 @@
         while todo.get(name):
             step(name)
 
-    g_parts = split(g_ref[...], 3)
-    for k, part in enumerate(g_parts):
-        ref[f"g{k}"][...] = part
     own_cols = pl.ds(pl.multiple_of(position * piece, piece), piece)
-    bases_own = b_ref[:, :, own_cols].reshape(levels * rank, piece)
     own_y = ref["y"].at[position]
 
-    def gram_of(first, last, width):
+    def products(left, parts):
+        return dot(left, parts[0], NN) + (dot(left, parts[1], NN) + dot(left, parts[2], NN))
+
+    def gram_of(solved, first, width):
+        own_y[first * rank : first * rank + solved.shape[0]] = solved
+        right = b_ref[:width, :, own_cols].reshape(width * rank, piece)
+        return sum(dot(part, right, NT) for part in reversed(split(solved, 3)))
+
+    def solved_of(first, last):
         left = b_ref[first:last].reshape((last - first) * rank, points)
-        solved = dot(left, g_parts[0], NN) + (
-            dot(left, g_parts[1], NN) + dot(left, g_parts[2], NN)
-        )
-        own_y[first * rank : last * rank] = solved
-        right = bases_own[: width * rank]
-        return sum(dot(part, right, NT) for part in reversed(split(solved, 3)))
-
-    ref["part_c"][...] = gram_of(0, 1, 1)
+        return products(left, [ref[f"g{k}"][...] for k in range(3)])
+
+    loads[0].wait()
+    solved = None
+    for c in range(CHUNKS):
+        loads[1 + c].wait()
+        if c == 1:
+            for load in loads[urgent:]:
+                load.start()
+        span = slice(c * chunk, (c + 1) * chunk)
+        parts = split(g_ref[span], 3)
+        for k, part in enumerate(parts):
+            ref[f"g{k}"][span] = part
+        value = products(b_ref[0, :, span], parts)
+        solved = value if c == 0 else solved + value
+    ref["part_c"][...] = gram_of(solved, 0, 1)
     pl.semaphore_wait(barrier, len(greeted))
     fold("c")
+    for load in loads[urgent : urgent + 2]:
+        load.wait()
     order = ord_ref[...]
 
     def one_hot(i, carry):
@@ -258,11 +307,6 @@
     for k in range(groups):
         ref["tree"][k] = tree[:, k * piece : (k + 1) * piece]
     scatter("c")
-    pieces = []
-    for peer in rhs_peers:
-        pieces.append(send(ref["tree"].at[peer], ref["cols"].at[position], (leaf, peer)))
-    ref["cols"][position] = ref["tree"][position]
-
     def part_store(gram, start, name, blocks):
         for k, (i, j) in enumerate(blocks):
             ref["part_" + name][k * rank : (k + 1) * rank] = gram[
@@ -270,10 +314,17 @@
             ]
 
     if levels > 1:
-        part_store(gram_of(1, 2, 2), 1, "a", direct["a"])
+        loads[urgent + 2].wait()
+        part_store(gram_of(solved_of(1, 2), 1, 2), 1, "a", direct["a"])
         fold("a")
+    ref["cols"][position] = ref["tree"][position]
+    copies = [
+        (ref["tree"].at[peer], ref["cols_get"].at[k], (leaf, peer))
+        for k, peer in enumerate(rhs_peers)
+    ]
+    pieces = Group(copies, ref["cols_get"])
     if levels > 2:
-        gram = gram_of(2, levels, levels)
+        gram = gram_of(solved_of(2, levels), 2, levels)
         later = {name: blocks for name, blocks in direct.items() if name not in "ca"}
         later |= slow
         for name, blocks in later.items():
@@ -287,8 +338,10 @@
     terms = []
 
     def term_part():
-        for copy in pieces:
-            copy.wait_recv()
+        pieces.wait_recv()
+        for k in range(groups - 1):
+            source = lax.rem(position + groups - 1 - k, groups)
+            ref["cols"][source] = ref["cols_get"][k]
         columns = ref["cols"][...].reshape(rows, piece)
         term = fine(columns, own_y[...], NT)
         for k in range(groups):
@@ -343,17 +396,29 @@
 
     solved_copies, relays = [], []
 
-    def solved_send():
-        for peer in across:
-            solved_copies.append(send(own_y, own_y, (leaf, peer)))
-        relays.append(send(own_y, own_y, (leaf, mate)))
+    def solved_across(first, last, place):
+        part = own_y.at[pl.ds(first * rank, (last - first) * rank)]
+        for k, peer in enumerate(across):
+            solved_copies.append(start(part, part, (leaf, peer), next(slots), place + k))
+
+    def solved_send(part):
+        early = 1
+        if part == 0:
+            solved_across(0, early, POOL)
+        else:
+            if early < levels:
+                solved_across(early, levels, POOL + len(across))
+            place = POOL + 2 * len(across)
+            relays.append(start(own_y, own_y, (leaf, mate), next(slots), place))
 
     def solved_relay():
-        for k, copy in enumerate(solved_copies):
+        for copy in solved_copies:
             copy.wait_recv()
+        for k in range(len(across)):
             source = lax.rem(position + groups - 2 * (k + 1), groups)
             slot = ref["y"].at[source]
-            relays.append(send(slot, slot, (leaf, mate)))
+            place = POOL + 2 * len(across) + 1 + k
+            relays.append(start(slot, slot, (leaf, mate), next(slots), place))
 
     def solved_done():
         for copy in relays:
@@ -425,9 +490,11 @@
                 change = fine(term_weights[h], below[h][j], NT)
                 span = slice(k * own_rows, (k + 1) * own_rows)
                 ref[f"tsend{h + 1}"][span] = term_value(h, j) - change
-            level_copies[h + 1, "terms"] = send(
-                ref[f"tsend{h + 1}"], ref[f"tget{h + 1}"], (other(leaf, 2 << h), position)
-            )
+
+    def terms_send(h):
+        level_copies[h + 1, "terms"] = send(
+            ref[f"tsend{h + 1}"], ref[f"tget{h + 1}"], (other(leaf, 2 << h), position)
+        )
 
     def level_change(h, block):
         i, j = block
@@ -453,27 +520,37 @@
     term_part()
     joined("c")
     hooks = {h: {} for h in range(levels)}
-    hooks[0] = {
-        1: [lambda: scatter("d")] if "d" in direct else [],
-        2: [term_cross],
-        4: [lambda: step("e1"), lambda: step("e2")],
-        6: [lambda: gather("a")] if "a" in direct else [],
-    }
+    if levels > 1:
+        hooks[0] = {5: [lambda: gather("a")]}
     if levels > 2:
+        hooks[0][1] = [lambda: scatter("d")]
+        hooks[0][3] = [term_cross]
+        hooks[0][4] = [lambda: step("e1"), lambda: step("e2")]
         hooks[1] = {
-            3: [lambda: step("e1"), lambda: step("e2")],
-            5: [term_joined, lambda: level_terms(0)],
-            7: [lambda: finish("e1")],
+            5: [lambda: step("e1")],
+            6: [term_joined, lambda: level_terms(0)],
+            7: [lambda: terms_send(0)],
         }
-    for h in range(2, levels):
-        hooks[h] = {}
+    else:
+        hooks[0][2] = [term_cross]
+    carry, partial = [None] * levels, [None] * levels
     for h in range(levels):
+        last = h == levels - 1
         if h:
             level_wait(h, "head")
             if h > 1:
                 finish(f"e{h}")
+        if last:
+            if h == 0:
+                term_sum()
+                solved_send(0)
+                solved_send(1)
+                plain_part()
+                plain_cross()
+                term_joined()
+            hooks[h] |= {1: [solved_relay], 5: [solved_done]}
         inverses[h] = inverse(block_value(h, (h, h)) + eye, hooks[h])
-        if h + 1 == levels:
+        if last:
             break
         if h == 0:
             joined("a")
@@ -489,9 +566,9 @@
         level_send(h + 1, "head", 0, rank)
         if h + 2 < levels:
             if h == 0:
+                solved_send(0)
                 gather("d")
-                step("e1")
-                step("e2")
+                plain_part()
                 joined("d")
             for i in range(h + 2, levels):
                 below[h][i] = block_value(h, (i, h))
@@ -499,34 +576,33 @@
             level_body(h)
         if h == 0:
             term_sum()
-            solved_send()
-            plain_part()
-        if h == levels - 2:
+            step("e2")
+            if levels == 2:
+                solved_send(0)
+            solved_send(1)
+            if levels == 2:
+                plain_part()
+        if h or levels == 2:
             if h == 0:
                 term_joined()
-                level_terms(0)
-            step("e2")
-        if h:
+            if h == levels - 2:
+                step("e2")
+                plain_cross()
             level_terms(h)
+            terms_send(h)
         if h == levels - 2:
-            hooks[h + 1] |= {0: [plain_cross], 1: [solved_relay], 6: [solved_done], 7: [plain_sum]}
-    if levels == 1:
-        term_sum()
-        solved_send()
-        plain_part()
-        term_joined()
-        plain_cross()
-        solved_relay()
-        plain_sum()
-        solved_done()
+            for k in reversed(range(levels - 1)):
+                carry[k] = weights[levels - 1, k]
+                partial[k] = term_weights[k]
+                for j in range(k + 1, levels - 1):
+                    carry[k] = carry[k] - fine(carry[j], weights[j, k], NN)
+                    partial[k] = partial[k] - fine(partial[j], weights[j, k], NN)
     level_terms(levels - 1)
-
-    coefficients = [None] * levels
-    for h in reversed(range(levels)):
-        value = term_weights[h]
-        for j in range(h + 1, levels):
-            value = value - fine(coefficients[j], weights[j, h], NN)
-        coefficients[h] = value
+    plain_sum()
+
+    coefficients = [term_weights[levels - 1] if h == levels - 1 else partial[h] for h in range(levels)]
+    for h in range(levels - 1):
+        coefficients[h] = coefficients[h] - fine(coefficients[levels - 1], carry[h], NN)
     stack = jnp.concatenate(split(jnp.concatenate(coefficients, 1), 2), 0)
     by_0 = dot(stack, ref["y0"][...], NN)
     by_1 = dot(stack[:own_rows], ref["y1"][...], NN)
@@ -534,7 +610,7 @@
     moved = dot(jnp.concatenate(split(tree_rows, 3), 0), ref["perm"][...], NT)
     out_ref[...] = moved[:own_rows] + (moved[own_rows : 2 * own_rows] + moved[2 * own_rows :])
 
-    for copy in started:
+    for copy in pool.values():
         copy.wait_send()
 
 
@@ -544,12 +620,17 @@
     width = levels * rank
     direct, slow = direct_units(levels), slow_units(levels)
     items = [
+        ("rs", pltpu.VMEM((own_rows, points), F32)),
+        ("g", pltpu.VMEM((points, piece), F32)),
+        ("b", pltpu.VMEM((levels, rank, points), BF16)),
+        ("ord", pltpu.VMEM((1, points), jnp.int32)),
         ("y", pltpu.VMEM((groups, width, piece), F32)),
         ("y0", pltpu.VMEM((width, points), BF16)),
         ("y1", pltpu.VMEM((width, points), BF16)),
         ("x", pltpu.VMEM((own_rows, points), F32)),
         ("tree", pltpu.VMEM((groups, own_rows, piece), F32)),
         ("cols", pltpu.VMEM((groups, own_rows, piece), F32)),
+        ("cols_get", pltpu.VMEM((groups - 1, own_rows, piece), F32)),
         ("plain", pltpu.VMEM((2, groups // 2, own_rows, points), F32)),
         ("plain_fold", pltpu.VMEM((groups // 2, own_rows, points), F32)),
         ("plain_chip", pltpu.VMEM((groups // 2, own_rows, points), F32)),
@@ -565,7 +646,7 @@
         ("g2", pltpu.VMEM((points, piece), BF16)),
         ("perm", pltpu.VMEM((points, points), BF16)),
     ]
-    count = 3 * groups + 4 * (levels - 1)
+    count = 6 + 3 * (groups // 2) - 2 + 4 * (levels - 1)
     for name, blocks in [*direct.items(), *slow.items()]:
         height = len(blocks) * rank
         items += [
@@ -574,14 +655,14 @@
             ("full_" + name, pltpu.VMEM((height, rank), F32)),
         ]
         if name in direct:
-            count += 2 + chips
+            count += 3
             items += [
                 ("chip_" + name, pltpu.VMEM((height // 2, rank), F32)),
                 ("peer_" + name, pltpu.VMEM((chips, height // 2, rank), F32)),
             ]
         else:
-            stages = len(stages_of(name, groups))
-            count += 2 + stages
+            stages = len(stages_of(name)) + chips
+            count += 2 + len(stages_of(name))
             items += [
                 ("pass_" + name, pltpu.VMEM((stages, height // 2, rank), F32)),
                 ("come_" + name, pltpu.VMEM((stages, height // 2, rank), F32)),
@@ -593,7 +674,7 @@
         height = (levels - h) * own_rows
         items.append((f"tsend{h}", pltpu.VMEM((height, rank), F32)))
         items.append((f"tget{h}", pltpu.VMEM((height, rank), F32)))
-    items.append(("sent", pltpu.SemaphoreType.DMA((count,))))
+    items.append(("sent", pltpu.SemaphoreType.DMA((POOL + 3 * (groups // 2) - 1,))))
     items.append(("received", pltpu.SemaphoreType.DMA((count,))))
     return items
 
@@ -616,8 +697,8 @@
     )
     return pl.pallas_call(
         functools.partial(kernel, cfg),
-        out_shape=jax.ShapeDtypeStruct((own_rows, points), F32),
-        in_specs=[pl.BlockSpec(memory_space=pltpu.VMEM)] * 4,
+        out_shape=pltpu.VMEM((own_rows, points), F32),
+        in_specs=[pl.BlockSpec(memory_space=pl.ANY)] * 4,
         out_specs=pl.BlockSpec(memory_space=pltpu.VMEM),
         scratch_shapes=[item for _, item in scratch_list(cfg)],
         compiler_params=pltpu.CompilerParams(collective_id=0, has_side_effects=True),

time: 39.4 us -> 36.7 us (0.931)
  Pallas kernels: 37.4 us -> 35.7 us
  local copies, waits for them, and re-layouts: 1.47 us -> 0.63 us
    pallas_call x1, Pallas kernels: 37.4 us -> 35.7 us  [local(): pl.pallas_call(functools.partial(kernel, cfg), out_shape=pltpu.VMEM((own_...]
    unnamed x1, local copies, waits for them, and re-layouts: 1.47 us -> 0.63 us
where the time goes in v3:
time: 36.7 us; the launch traced here: 36.3 us
  Pallas kernels  35.7 us (97%)
  local copies, waits for them, and re-layouts  0.63 us (2%)
    pallas_call x1, Pallas kernels, local(): pl.pallas_call(functools.partial(kernel, cfg), out_shape=pltpu.VMEM((own_...  35.7 us

profile of v3, /device:TPU:0, one launch (start us, length us, event | category | flops | bytes accessed | tf_op | source)
XLA Modules:
  0.0 36.3 jit_solution(12001536920518564548)
XLA Ops:
  0.0 35.7 %tree_solve.1 = f32[16,1024]{1,0:T(8,128)S(1)} custom-call(f32[16,1024]{1,0:T(8,128)} %rs_hbm.1, f32[1024,256]{1,0:T(8,128)} %g_hbm.1, bf16[3,128,1024]{2,1,0:T(8,128)(2,1)} %b_hbm.1, s32[1,1024]{1,0:T(1,128)} %ord_hbm.1), custom_call_target="tpu_custom_call" | custom-call | tf_op jit(solution)/shard_map/tree_solve/pallas_call | solution.py:698
  35.7 0.6 %copy.6 = f32[16,1024]{1,0:T(8,128)} copy(f32[16,1024]{1,0:T(8,128)S(1)} %tree_solve.1) | data formatting | bytes 131072

commit v4 on v3

--- a/solution.py
+++ b/solution.py
@@ -15,6 +15,8 @@
 PANEL = 16
 CHUNKS = 4
 POOL = 12
+ROWS, LANES = 8, 128
+RADIX = 32
 
 
 def split(value, pieces):
@@ -89,6 +91,57 @@
     return [(first, first)] + later
 
 
+def permute(value, index):
+    tile = (ROWS, LANES)
+    width = value.shape[1]
+    bands = []
+    for top in range(0, value.shape[0], ROWS):
+        out = []
+        for left in range(0, width, LANES):
+            own = jnp.broadcast_to(index[:, left : left + LANES], tile)
+            lane, block = lax.rem(own, LANES), lax.div(own, LANES)
+            taken = None
+            for source in range(width // LANES):
+                part = value[top : top + ROWS, source * LANES : (source + 1) * LANES]
+                part = jnp.take_along_axis(part, lane, axis=1)
+                taken = part if taken is None else jnp.where(block == source, part, taken)
+            out.append(taken)
+        bands.append(jnp.concatenate(out, 1))
+    return jnp.concatenate(bands, 0)
+
+
+def layout(blocks, rank):
+    spans, start = {}, 0
+    for i, j in blocks:
+        stop = start + (rank // 8 * 5 if i == j else rank)
+        spans[i, j] = slice(start, stop)
+        start = stop
+    return spans, start
+
+
+def pack(matrix):
+    quarter = matrix.shape[0] // 4
+    lane = lax.broadcasted_iota(jnp.int32, (1, 4 * quarter), 1)
+    zero, one, two, three = (matrix[k * quarter : (k + 1) * quarter] for k in range(4))
+    two = jnp.where(lane < 3 * quarter, two, pltpu.roll(zero, 3 * quarter, 1))
+    low, high = one[: quarter // 2], one[quarter // 2 :]
+    one = jnp.where(lane < 2 * quarter, low, pltpu.roll(high, 2 * quarter, 1))
+    return jnp.concatenate([three, two, one], 0)
+
+
+def unpack(packed):
+    quarter = packed.shape[1] // 4
+    three, two = packed[:quarter], packed[quarter : 2 * quarter]
+    low = packed[2 * quarter :]
+    lower = jnp.concatenate(
+        [pltpu.roll(two, quarter, 1), low, pltpu.roll(low, 2 * quarter, 1), two, three], 0
+    )
+    upper = lower.T
+    row = lax.broadcasted_iota(jnp.int32, (4 * quarter, 4 * quarter), 0)
+    lane = lax.broadcasted_iota(jnp.int32, (4 * quarter, 4 * quarter), 1)
+    return jnp.where(lane // quarter > row // quarter, upper, lower)
+
+
 def direct_units(levels):
     units = {"c": [(0, 0)]}
     if levels > 1:
@@ -107,9 +160,11 @@
     return units
 
 
-def stages_of(name):
+def stages_of(name, groups):
     column = int(name[1:])
-    return [1 << h for h in range(1, column + 1)] + [None]
+    stages = [(1 << h, 0) for h in range(1, column + 1)]
+    stages += [(0, 1 << k) for k in range(1, groups.bit_length() - 1)]
+    return stages + [(1, 0)]
 
 
 def other(index, bit):
@@ -225,29 +280,24 @@
         flying[name].wait_recv()
 
     def slow_step(name, stage):
-        stages = stages_of(name)
+        stages = stages_of(name, groups)
         if stage == 0:
             total = folded(name)
         else:
             total = ref["pass_" + name][stage - 1]
             flying[name].wait_recv()
-            for k in range(1 if stages[stage - 1] else len(chips)):
-                total = total + ref["come_" + name][stage - 1 + k]
+            total = total + ref["come_" + name][stage - 1]
         if stage == len(stages):
             join(name, total)
             return
         ref["pass_" + name][stage] = total
-        if stages[stage] is None:
-            targets = chips
-        else:
-            targets = [(other(leaf, stages[stage]), position)]
-        own, landed = ref["pass_" + name].at[stage], ref["come_" + name]
-        copies = [(own, landed.at[stage + k], target) for k, target in enumerate(targets)]
-        flying[name] = Group(copies, landed.at[pl.ds(stage, len(targets))])
+        leaf_bit, rhs_bit = stages[stage]
+        target = (other(leaf, leaf_bit), other(position, rhs_bit))
+        flying[name] = send(ref["pass_" + name].at[stage], ref["come_" + name].at[stage], target)
 
     todo = {}
     for name in slow:
-        count = len(stages_of(name))
+        count = len(stages_of(name, groups))
         todo[name] = [functools.partial(slow_step, name, k) for k in range(count + 1)]
         todo[name].append(functools.partial(joined, name))
 
@@ -279,8 +329,10 @@
     solved = None
     for c in range(CHUNKS):
         loads[1 + c].wait()
-        if c == 1:
-            for load in loads[urgent:]:
+        if c == CHUNKS // 2:
+            loads[-1].start()
+        if c == CHUNKS - 1:
+            for load in loads[urgent : urgent + 2]:
                 load.start()
         span = slice(c * chunk, (c + 1) * chunk)
         parts = split(g_ref[span], 3)
@@ -288,35 +340,46 @@
             ref[f"g{k}"][span] = part
         value = products(b_ref[0, :, span], parts)
         solved = value if c == 0 else solved + value
-    ref["part_c"][...] = gram_of(solved, 0, 1)
+    ref["part_c"][...] = pack(gram_of(solved, 0, 1))
     pl.semaphore_wait(barrier, len(greeted))
     fold("c")
-    for load in loads[urgent : urgent + 2]:
-        load.wait()
-    order = ord_ref[...]
-
-    def one_hot(i, carry):
-        start = pl.multiple_of(i * rank, rank)
-        index = lax.broadcasted_iota(jnp.int32, (rank, points), 0) + start
-        ref["perm"][pl.ds(start, rank), :] = jnp.where(index == order, 1.0, 0.0).astype(BF16)
-        return carry
-
-    lax.fori_loop(0, points // rank, one_hot, 0)
-    moved = dot(jnp.concatenate(split(rs_ref[...], 3), 0), ref["perm"][...], NN)
-    tree = (moved[:own_rows] + moved[own_rows : 2 * own_rows]) + moved[2 * own_rows :]
-    for k in range(groups):
-        ref["tree"][k] = tree[:, k * piece : (k + 1) * piece]
-    scatter("c")
+
+    def arrange():
+        for load in loads[urgent : urgent + 2]:
+            load.wait()
+        tree = permute(rs_ref[...], ord_ref[...])
+        for k in range(groups):
+            ref["tree"][k] = tree[:, k * piece : (k + 1) * piece]
+
+    def invert_order():
+        order = ord_ref[...]
+
+        def one_hot(i, carry):
+            start = pl.multiple_of(i * rank, rank)
+            index = lax.broadcasted_iota(jnp.int32, (rank, points), 0) + start
+            ref["perm"][pl.ds(start, rank), :] = jnp.where(index == order, 1.0, 0.0).astype(BF16)
+            return carry
+
+        lax.fori_loop(0, points // rank, one_hot, 0)
+        row = lax.broadcasted_iota(jnp.int32, (2 * ROWS, points), 0)
+        lane = lax.broadcasted_iota(jnp.int32, (2 * ROWS, points), 1)
+        digits = jnp.where(row == 0, lax.div(lane, RADIX), lax.rem(lane, RADIX))
+        found = dot(digits.astype(F32).astype(BF16), ref["perm"][...], NT)
+        ref["back"][...] = (found[:1] * RADIX + found[1:2]).astype(jnp.int32)
+
     def part_store(gram, start, name, blocks):
-        for k, (i, j) in enumerate(blocks):
-            ref["part_" + name][k * rank : (k + 1) * rank] = gram[
-                (i - start) * rank : (i - start + 1) * rank, j * rank : (j + 1) * rank
-            ]
+        for (i, j), span in layout(blocks, rank)[0].items():
+            block = gram[(i - start) * rank : (i - start + 1) * rank, j * rank : (j + 1) * rank]
+            ref["part_" + name][span] = pack(block) if i == j else block
 
     if levels > 1:
         loads[urgent + 2].wait()
-        part_store(gram_of(solved_of(1, 2), 1, 2), 1, "a", direct["a"])
+        solved = solved_of(1, 2)
+    scatter("c")
+    if levels > 1:
+        part_store(gram_of(solved, 1, 2), 1, "a", direct["a"])
         fold("a")
+    arrange()
     ref["cols"][position] = ref["tree"][position]
     copies = [
         (ref["tree"].at[peer], ref["cols_get"].at[k], (leaf, peer))
@@ -397,17 +460,16 @@
     solved_copies, relays = [], []
 
     def solved_across(first, last, place):
-        part = own_y.at[pl.ds(first * rank, (last - first) * rank)]
+        part = own_y.at[pl.ds(first, last - first)]
         for k, peer in enumerate(across):
             solved_copies.append(start(part, part, (leaf, peer), next(slots), place + k))
 
     def solved_send(part):
-        early = 1
+        early = rank // 2
         if part == 0:
             solved_across(0, early, POOL)
         else:
-            if early < levels:
-                solved_across(early, levels, POOL + len(across))
+            solved_across(early, levels * rank, POOL + len(across))
             place = POOL + 2 * len(across)
             relays.append(start(own_y, own_y, (leaf, mate), next(slots), place))
 
@@ -433,20 +495,16 @@
     ).astype(F32)
     linear = {}
     for name, blocks in [*direct.items(), *slow.items()]:
-        for k, block in enumerate(blocks):
-            linear[block] = (name, k * rank)
-    place = {}
-    for h in range(1, levels):
-        for k, block in enumerate(blocks_of(levels, h)):
-            place[h, block] = k * rank
+        for block, span in layout(blocks, rank)[0].items():
+            linear[block] = (name, span)
+    places = [layout(blocks_of(levels, h), rank)[0] for h in range(levels)]
 
     def linear_value(block):
-        name, start = linear[block]
-        return ref["full_" + name][start : start + rank]
+        name, span = linear[block]
+        return ref["full_" + name][span]
 
     def carried(h, block):
-        start = place[h, block]
-        span = slice(start, start + rank)
+        span = places[h][block]
         return ref[f"send{h}"][span] + ref[f"get{h}"][span]
 
     def block_value(h, block):
@@ -484,10 +542,11 @@
     def level_terms(h):
         if h:
             level_wait(h, "terms")
-        term_weights[h] = fine(term_value(h, h), inverses[h], NN)
+        own = term_value(h, h)
+        term_weights[h] = fine(own, inverses[h], NN)
         if h + 1 < levels:
             for k, j in enumerate(range(h + 1, levels)):
-                change = fine(term_weights[h], below[h][j], NT)
+                change = fine(own, weights[j, h], NT)
                 span = slice(k * own_rows, (k + 1) * own_rows)
                 ref[f"tsend{h + 1}"][span] = term_value(h, j) - change
 
@@ -499,20 +558,33 @@
     def level_change(h, block):
         i, j = block
         change = fine(weights[i, h], below[h][j], NT)
+        if i == j:
+            change = pack(change)
         if block == (1, 1):
             return linear_value(block) - change
         return carried(h, block) - change if h else -change
 
-    def level_body(h):
+    def level_span(h, first, last):
+        return [(block, places[h][block]) for block in blocks_of(levels, h)[first:last]]
+
+    def level_column(h):
         level_wait(h, "rest")
-        target = ref[f"send{h + 1}"]
-        blocks = blocks_of(levels, h + 1)
-        split_at = levels - h - 1
-        for part, first, last in (("column", 1, split_at), ("rest", split_at, len(blocks))):
-            for k in range(first, last):
-                target[k * rank : (k + 1) * rank] = level_change(h, blocks[k])
-            if last > first:
-                level_send(h + 1, part, first * rank, last * rank)
+        spans = level_span(h + 1, 1, levels - h - 1)
+        for (i, j), span in spans:
+            change = fine(below[h][i], weights[j, h], NT)
+            ref[f"send{h + 1}"][span] = carried(h, (i, j)) - change if h else -change
+        level_send(h + 1, "column", spans[0][1].start, spans[-1][1].stop)
+
+    def level_rest(h):
+        for i in range(h + 2, levels):
+            weights[i, h] = fine(below[h][i], inverses[h], NN)
+        for block, span in level_span(h + 1, levels - h - 1, None):
+            ref[f"send{h + 1}"][span] = level_change(h, block)
+
+    def level_rest_send(h):
+        spans = level_span(h + 1, levels - h - 1, None)
+        level_send(h + 1, "rest", spans[0][1].start, spans[-1][1].stop)
+
 
     for name in slow:
         step(name)
@@ -527,8 +599,8 @@
         hooks[0][3] = [term_cross]
         hooks[0][4] = [lambda: step("e1"), lambda: step("e2")]
         hooks[1] = {
-            5: [lambda: step("e1")],
-            6: [term_joined, lambda: level_terms(0)],
+            3: [lambda: step("e1")],
+            6: [lambda: step("e2"), term_joined, lambda: level_terms(0)],
             7: [lambda: terms_send(0)],
         }
     else:
@@ -548,8 +620,10 @@
                 plain_part()
                 plain_cross()
                 term_joined()
-            hooks[h] |= {1: [solved_relay], 5: [solved_done]}
-        inverses[h] = inverse(block_value(h, (h, h)) + eye, hooks[h])
+                solved_relay()
+                invert_order()
+            hooks[h][7] = [solved_done]
+        inverses[h] = inverse(unpack(block_value(h, (h, h))) + eye, hooks[h])
         if last:
             break
         if h == 0:
@@ -562,25 +636,32 @@
         weights[h + 1, h] = fine(first, inverses[h], NN)
         if h:
             level_wait(h, "rest")
-        ref[f"send{h + 1}"][:rank] = level_change(h, (h + 1, h + 1))
-        level_send(h + 1, "head", 0, rank)
+        span = places[h + 1][h + 1, h + 1]
+        ref[f"send{h + 1}"][span] = level_change(h, (h + 1, h + 1))
+        level_send(h + 1, "head", span.start, span.stop)
         if h + 2 < levels:
             if h == 0:
                 solved_send(0)
                 gather("d")
+                step("e1")
                 plain_part()
+                step("e2")
+                solved_send(1)
                 joined("d")
             for i in range(h + 2, levels):
                 below[h][i] = block_value(h, (i, h))
-                weights[i, h] = fine(below[h][i], inverses[h], NN)
-            level_body(h)
+            level_column(h)
+            if h == 0:
+                hooks[1][1] = [lambda: level_rest(0)]
+                hooks[1][2] = [lambda: level_rest_send(0)]
+            else:
+                level_rest(h)
+                level_rest_send(h)
         if h == 0:
             term_sum()
-            step("e2")
             if levels == 2:
                 solved_send(0)
-            solved_send(1)
-            if levels == 2:
+                solved_send(1)
                 plain_part()
         if h or levels == 2:
             if h == 0:
@@ -588,6 +669,7 @@
             if h == levels - 2:
                 step("e2")
                 plain_cross()
+                invert_order()
             level_terms(h)
             terms_send(h)
         if h == levels - 2:
@@ -597,6 +679,7 @@
                 for j in range(k + 1, levels - 1):
                     carry[k] = carry[k] - fine(carry[j], weights[j, k], NN)
                     partial[k] = partial[k] - fine(partial[j], weights[j, k], NN)
+            solved_relay()
     level_terms(levels - 1)
     plain_sum()
 
@@ -607,8 +690,7 @@
     by_0 = dot(stack, ref["y0"][...], NN)
     by_1 = dot(stack[:own_rows], ref["y1"][...], NN)
     tree_rows = ref["x"][...] - (by_0[:own_rows] + (by_0[own_rows:] + by_1))
-    moved = dot(jnp.concatenate(split(tree_rows, 3), 0), ref["perm"][...], NT)
-    out_ref[...] = moved[:own_rows] + (moved[own_rows : 2 * own_rows] + moved[2 * own_rows :])
+    out_ref[...] = permute(tree_rows, ref["back"][...])
 
     for copy in pool.values():
         copy.wait_send()
@@ -645,10 +727,11 @@
         ("g1", pltpu.VMEM((points, piece), BF16)),
         ("g2", pltpu.VMEM((points, piece), BF16)),
         ("perm", pltpu.VMEM((points, points), BF16)),
+        ("back", pltpu.VMEM((1, points), jnp.int32)),
     ]
     count = 6 + 3 * (groups // 2) - 2 + 4 * (levels - 1)
     for name, blocks in [*direct.items(), *slow.items()]:
-        height = len(blocks) * rank
+        height = layout(blocks, rank)[1]
         items += [
             ("part_" + name, pltpu.VMEM((height, rank), F32)),
             ("fold_" + name, pltpu.VMEM((height // 2, rank), F32)),
@@ -661,14 +744,14 @@
                 ("peer_" + name, pltpu.VMEM((chips, height // 2, rank), F32)),
             ]
         else:
-            stages = len(stages_of(name)) + chips
-            count += 2 + len(stages_of(name))
+            stages = len(stages_of(name, groups))
+            count += 2 + stages
             items += [
                 ("pass_" + name, pltpu.VMEM((stages, height // 2, rank), F32)),
                 ("come_" + name, pltpu.VMEM((stages, height // 2, rank), F32)),
             ]
     for h in range(1, levels):
-        height = len(blocks_of(levels, h)) * rank
+        height = layout(blocks_of(levels, h), rank)[1]
         items.append((f"send{h}", pltpu.VMEM((height, rank), F32)))
         items.append((f"get{h}", pltpu.VMEM((height, rank), F32)))
         height = (levels - h) * own_rows

time: 36.7 us -> 32.7 us (0.89)
  Pallas kernels: 35.7 us -> 31.9 us
    pallas_call x1, Pallas kernels: 35.7 us -> 31.9 us  [local(): pl.pallas_call(functools.partial(kernel, cfg), out_shape=pltpu.VMEM((own_...]
where the time goes in v4:
time: 32.7 us; the launch traced here: 32.6 us
  Pallas kernels  31.9 us (98%)
  local copies, waits for them, and re-layouts  0.63 us (2%)
    pallas_call x1, Pallas kernels, local(): pl.pallas_call(functools.partial(kernel, cfg), out_shape=pltpu.VMEM((own_...  31.9 us

profile of v4, /device:TPU:0, one launch (start us, length us, event | category | flops | bytes accessed | tf_op | source)
XLA Modules:
  0.0 32.6 jit_solution(15056989912194248083)
XLA Ops:
  0.0 31.9 %tree_solve.1 = f32[16,1024]{1,0:T(8,128)S(1)} custom-call(f32[16,1024]{1,0:T(8,128)} %rs_hbm.1, f32[1024,256]{1,0:T(8,128)} %g_hbm.1, bf16[3,128,1024]{2,1,0:T(8,128)(2,1)} %b_hbm.1, s32[1,1024]{1,0:T(1,128)} %ord_hbm.1), custom_call_target="tpu_custom_call" | custom-call | tf_op jit(solution)/shard_map/tree_solve/pallas_call | solution.py:781
  31.9 0.6 %copy.6 = f32[16,1024]{1,0:T(8,128)} copy(f32[16,1024]{1,0:T(8,128)S(1)} %tree_solve.1) | data formatting | bytes 131072

commit v5 on v4

--- a/solution.py
+++ b/solution.py
@@ -36,6 +36,12 @@
     return lax.dot_general(
         left, right, dims, precision=lax.Precision.HIGHEST, preferred_element_type=F32
     )
+
+
+def coarse(left, right, dims):
+    first, second = split(left, 2)
+    upper, lower = split(right, 2)
+    return dot(first, upper, dims) + (dot(second, upper, dims) + dot(first, lower, dims))
 
 
 def inverse(matrix, hooks):
@@ -69,7 +75,7 @@
                 pivot = columns[j][k : k + 1] * scale
                 columns[j] = jnp.where(at, 0.0, columns[j]) - factor * pivot
         padded = jnp.concatenate([zero] * i + [panel] + [zero] * (count - 1 - i), 0)
-        update = fine(jnp.concatenate(panels, 0), padded, NN)
+        update = coarse(jnp.concatenate(panels, 0), padded, NN)
         if ahead:
             change = next_columns[0] * panel[0:1]
             for k in range(1, PANEL):
@@ -543,10 +549,10 @@
         if h:
             level_wait(h, "terms")
         own = term_value(h, h)
-        term_weights[h] = fine(own, inverses[h], NN)
+        term_weights[h] = coarse(own, inverses[h], NN)
         if h + 1 < levels:
             for k, j in enumerate(range(h + 1, levels)):
-                change = fine(own, weights[j, h], NT)
+                change = coarse(own, weights[j, h], NT)
                 span = slice(k * own_rows, (k + 1) * own_rows)
                 ref[f"tsend{h + 1}"][span] = term_value(h, j) - change
 
@@ -557,7 +563,7 @@
 
     def level_change(h, block):
         i, j = block
-        change = fine(weights[i, h], below[h][j], NT)
+        change = coarse(weights[i, h], below[h][j], NT)
         if i == j:
             change = pack(change)
         if block == (1, 1):
@@ -571,13 +577,13 @@
         level_wait(h, "rest")
         spans = level_span(h + 1, 1, levels - h - 1)
         for (i, j), span in spans:
-            change = fine(below[h][i], weights[j, h], NT)
+            change = coarse(below[h][i], weights[j, h], NT)
             ref[f"send{h + 1}"][span] = carried(h, (i, j)) - change if h else -change
         level_send(h + 1, "column", spans[0][1].start, spans[-1][1].stop)
 
     def level_rest(h):
         for i in range(h + 2, levels):
-            weights[i, h] = fine(below[h][i], inverses[h], NN)
+            weights[i, h] = coarse(below[h][i], inverses[h], NN)
         for block, span in level_span(h + 1, levels - h - 1, None):
             ref[f"send{h + 1}"][span] = level_change(h, block)
 
@@ -600,8 +606,8 @@
         hooks[0][4] = [lambda: step("e1"), lambda: step("e2")]
         hooks[1] = {
             3: [lambda: step("e1")],
-            6: [lambda: step("e2"), term_joined, lambda: level_terms(0)],
-            7: [lambda: terms_send(0)],
+            5: [lambda: step("e2"), term_joined, lambda: level_terms(0)],
+            6: [lambda: terms_send(0)],
         }
     else:
         hooks[0][2] = [term_cross]
@@ -633,7 +639,7 @@
             finish(f"e{h}")
         first = block_value(h, (h + 1, h))
         below[h] = {h + 1: first}
-        weights[h + 1, h] = fine(first, inverses[h], NN)
+        weights[h + 1, h] = coarse(first, inverses[h], NN)
         if h:
             level_wait(h, "rest")
         span = places[h + 1][h + 1, h + 1]
@@ -685,7 +691,7 @@
 
     coefficients = [term_weights[levels - 1] if h == levels - 1 else partial[h] for h in range(levels)]
     for h in range(levels - 1):
-        coefficients[h] = coefficients[h] - fine(coefficients[levels - 1], carry[h], NN)
+        coefficients[h] = coefficients[h] - coarse(coefficients[levels - 1], carry[h], NN)
     stack = jnp.concatenate(split(jnp.concatenate(coefficients, 1), 2), 0)
     by_0 = dot(stack, ref["y0"][...], NN)
     by_1 = dot(stack[:own_rows], ref["y1"][...], NN)
@@ -729,7 +735,7 @@
         ("perm", pltpu.VMEM((points, points), BF16)),
         ("back", pltpu.VMEM((1, points), jnp.int32)),
     ]
-    count = 6 + 3 * (groups // 2) - 2 + 4 * (levels - 1)
+    count = 6 + 3 * (groups // 2) - 2 + 4 * (levels - 1) - 2 * (levels > 1)
     for name, blocks in [*direct.items(), *slow.items()]:
         height = layout(blocks, rank)[1]
         items += [

time: 32.7 us -> 31.6 us (0.966)
  Pallas kernels: 31.9 us -> 30.8 us
    pallas_call x1, Pallas kernels: 31.9 us -> 30.8 us  [local(): pl.pallas_call(functools.partial(kernel, cfg), out_shape=pltpu.VMEM((own_...]
where the time goes in v5:
time: 31.6 us; the launch traced here: 31.5 us
  Pallas kernels  30.8 us (97%)
  local copies, waits for them, and re-layouts  0.63 us (2%)
    pallas_call x1, Pallas kernels, local(): pl.pallas_call(functools.partial(kernel, cfg), out_shape=pltpu.VMEM((own_...  30.8 us
    unnamed x1, local copies, waits for them, and re-layouts  0.63 us

profile of v5, /device:TPU:0, one launch (start us, length us, event | category | flops | bytes accessed | tf_op | source)
XLA Modules:
  0.0 31.5 jit_solution(5495162929882640607)
XLA Ops:
  0.0 30.8 %tree_solve.1 = f32[16,1024]{1,0:T(8,128)S(1)} custom-call(f32[16,1024]{1,0:T(8,128)} %rs_hbm.1, f32[1024,256]{1,0:T(8,128)} %g_hbm.1, bf16[3,128,1024]{2,1,0:T(8,128)(2,1)} %b_hbm.1, s32[1,1024]{1,0:T(1,128)} %ord_hbm.1), custom_call_target="tpu_custom_call" | custom-call | tf_op jit(solution)/shard_map/tree_solve/pallas_call | solution.py:787
  30.8 0.6 %copy.6 = f32[16,1024]{1,0:T(8,128)} copy(f32[16,1024]{1,0:T(8,128)S(1)} %tree_solve.1) | data formatting | bytes 131072

commit v6 on v5

--- a/solution.py
+++ b/solution.py
@@ -320,16 +320,16 @@
     own_y = ref["y"].at[position]
 
     def products(left, parts):
-        return dot(left, parts[0], NN) + (dot(left, parts[1], NN) + dot(left, parts[2], NN))
+        return dot(left, parts[0], NN) + dot(left, parts[1], NN)
 
     def gram_of(solved, first, width):
         own_y[first * rank : first * rank + solved.shape[0]] = solved
         right = b_ref[:width, :, own_cols].reshape(width * rank, piece)
-        return sum(dot(part, right, NT) for part in reversed(split(solved, 3)))
+        return sum(dot(part, right, NT) for part in reversed(split(solved, 2)))
 
     def solved_of(first, last):
         left = b_ref[first:last].reshape((last - first) * rank, points)
-        return products(left, [ref[f"g{k}"][...] for k in range(3)])
+        return products(left, [ref[f"g{k}"][...] for k in range(2)])
 
     loads[0].wait()
     solved = None

time: 31.6 us -> 31.5 us (level)
  no operation moved by 1% of the time
where the time goes in v6:
time: 31.5 us; the launch traced here: 31.4 us
  Pallas kernels  30.8 us (98%)
  local copies, waits for them, and re-layouts  0.63 us (2%)
    pallas_call x1, Pallas kernels, local(): pl.pallas_call(functools.partial(kernel, cfg), out_shape=pltpu.VMEM((own_...  30.8 us
    unnamed x1, local copies, waits for them, and re-layouts  0.63 us

profile of v6, /device:TPU:0, one launch (start us, length us, event | category | flops | bytes accessed | tf_op | source)
XLA Modules:
  0.0 31.4 jit_solution(8814703005851701585)
XLA Ops:
  0.0 30.8 %tree_solve.1 = f32[16,1024]{1,0:T(8,128)S(1)} custom-call(f32[16,1024]{1,0:T(8,128)} %rs_hbm.1, f32[1024,256]{1,0:T(8,128)} %g_hbm.1, bf16[3,128,1024]{2,1,0:T(8,128)(2,1)} %b_hbm.1, s32[1,1024]{1,0:T(1,128)} %ord_hbm.1), custom_call_target="tpu_custom_call" | custom-call | tf_op jit(solution)/shard_map/tree_solve/pallas_call | solution.py:787
  30.8 0.6 %copy.6 = f32[16,1024]{1,0:T(8,128)} copy(f32[16,1024]{1,0:T(8,128)S(1)} %tree_solve.1) | data formatting | bytes 131072
